TPU v7x, 32 devices: a whole 2x2x4 slice. The times are simulated.
32 devices in a mesh: row: 8 (over z, x), col: 4 (over y, core).
Axes of the slice: x: 2, y: 2, z: 4, core: 2. Of those that a mesh axis runs over, the one named last changes fastest.
Arguments:
- p_values: bfloat16 [96, 512, 128], P('row', 'col'), may hold values from -0.8984375 to 0.8984375
- p_where: int32 [96, 8], P('row', 'col'), may hold values from 0 to 63, as said below
- p_count: int32 [8, 4], P('row', 'col'), may hold values from 6 to 12, as said below
- h_values: bfloat16 [96, 512, 128], P('row', 'col'), may hold values from -3 to 3
- h_where: int32 [96, 8], P('row', 'col'), may hold values from 0 to 63, as said below
- h_count: int32 [8, 4], P('row', 'col'), may hold values from 6 to 12, as said below
Outputs:
- ph_values: bfloat16 [96, 512, 128], P('row', 'col')
- php_values: bfloat16 [96, 512, 128], P('row', 'col')
- energy: float32 [], replicated
Inputs may be any that keep to these rules, and one draw needn't show every extreme that they name: `p_where`: the 12 slots of the device of row index i and column index j name distinct blocks of its own tile: block rows i * 8 to i * 8 + 7 and the j-th of 4 equal ranges of block columns. `h_where`: as for p_where. `p_count`: some device has all 12 slots live. `h_count`: some device has all 12 slots live.
All inputs are finite; a program needn't handle non-finite values.
Results may differ from a plain program's by a relative error of at most 0.0049.
Values may be sent and summed in bfloat16 or wider, within the bound.
A program may use at most 64 MiB of HBM per device.

v0:
```python
import jax
import jax.numpy as jnp
from jax import lax
from jax.sharding import PartitionSpec as P

TILE = 8


def contribute(total_sum, left_tile, right_tile, band_index, out_where):
    left_vals, left_where, left_count = left_tile
    right_vals, right_where, right_count = right_tile
    slot_count = left_vals.shape[0]
    inner_blocks = band_index * TILE + jnp.arange(TILE, dtype=jnp.int32)
    left_live = jnp.arange(slot_count, dtype=jnp.int32) < left_count[0, 0]
    right_live = jnp.arange(slot_count, dtype=jnp.int32) < right_count[0, 0]
    match_left = (
        (left_where[None, None, :, 0] == out_where[:, None, None, 0])
        & (left_where[None, None, :, 1] == inner_blocks[None, :, None])
        & left_live[None, None, :]
    )
    match_right = (
        (right_where[None, None, :, 1] == out_where[:, None, None, 1])
        & (right_where[None, None, :, 0] == inner_blocks[None, :, None])
        & right_live[None, None, :]
    )
    pick_left = jnp.argmax(match_left.astype(jnp.int32), axis=2)
    pick_right = jnp.argmax(match_right.astype(jnp.int32), axis=2)
    has_left = jnp.any(match_left, axis=2)
    has_right = jnp.any(match_right, axis=2)
    nothing = jnp.zeros((), jnp.bfloat16)

    def slot_product(items):
        left_pick, left_has, right_pick, right_has = items
        row_blocks = jnp.where(left_has[:, None, None], left_vals[left_pick], nothing)
        col_blocks = jnp.where(right_has[:, None, None], right_vals[right_pick], nothing)
        return jnp.einsum("kxy,kyz->xz", row_blocks, col_blocks, preferred_element_type=jnp.float32)

    return total_sum + lax.map(slot_product, (pick_left, has_left, pick_right, has_right))


def pick_tile(gathered, owner, slot_count):
    all_vals, all_where, all_count = gathered
    start = (owner * slot_count).astype(jnp.int32)
    vals = lax.dynamic_slice_in_dim(all_vals, start, slot_count, 0)
    where = lax.dynamic_slice_in_dim(all_where, start, slot_count, 0)
    count = lax.dynamic_slice_in_dim(all_count, owner.astype(jnp.int32), 1, 0)
    return (vals, where, count)


def multiply(left_tile, right_tile, out_where):
    rows_count = lax.axis_size("row")
    cols_count = lax.axis_size("col")
    band_ratio = rows_count // cols_count
    slot_count = out_where.shape[0]
    block_size = left_tile[0].shape[1]
    zero_sum = jnp.zeros((slot_count, block_size, block_size), jnp.float32)
    left_all = (
        lax.all_gather(left_tile[0], "col", axis=0, tiled=True),
        lax.all_gather(left_tile[1], "col", axis=0, tiled=True),
        lax.all_gather(left_tile[2], "col", axis=0, tiled=True),
    )
    right_all = (
        lax.all_gather(right_tile[0], "row", axis=0, tiled=True),
        lax.all_gather(right_tile[1], "row", axis=0, tiled=True),
        lax.all_gather(right_tile[2], "row", axis=0, tiled=True),
    )

    def band_step(band_index, total_sum):
        left_here = pick_tile(left_all, band_index // band_ratio, slot_count)
        right_here = pick_tile(right_all, band_index, slot_count)
        return contribute(total_sum, left_here, right_here, band_index, out_where)

    return lax.fori_loop(0, rows_count, band_step, zero_sum)


def per_device(p_values, p_where, p_count, h_values, h_where, h_count):
    slot_count = p_values.shape[0]
    live_slots = jnp.arange(slot_count, dtype=jnp.int32) < p_count[0, 0]
    density_tile = (p_values, p_where, p_count)
    first_sum = multiply(density_tile, (h_values, h_where, h_count), p_where)
    first_sum = jnp.where(live_slots[:, None, None], first_sum, jnp.float32(0.0))
    traces = jnp.trace(first_sum, axis1=1, axis2=2)
    diagonal = live_slots & (p_where[:, 0] == p_where[:, 1])
    local_energy = jnp.sum(jnp.where(diagonal, traces, jnp.float32(0.0)))
    ph_values = first_sum.astype(jnp.bfloat16)
    second_sum = multiply((ph_values, p_where, p_count), density_tile, p_where)
    php_values = jnp.where(live_slots[:, None, None], second_sum, jnp.float32(0.0)).astype(
        jnp.bfloat16
    )
    energy = lax.psum(local_energy, ("row", "col"))
    return (ph_values, php_values, energy)


def solution(mesh):
    placed = (
        P("row", "col", None),
        P("row", "col"),
        P("row", "col"),
        P("row", "col", None),
        P("row", "col"),
        P("row", "col"),
    )
    return jax.shard_map(
        per_device,
        mesh=mesh,
        in_specs=placed,
        out_specs=(P("row", "col", None), P("row", "col", None), P()),
        check_vma=False,
    )
```

profile of v0, /device:TPU:12, one launch (start us, length us, event | category | flops | bytes accessed | tf_op | source)
XLA Modules:
  0.0 583.5 jit_solution(3601513037107337282)
XLA Ops:
  10.1 1.2 dynamic-slice.1
  11.3 1.2 dynamic-slice
  13.9 4.3 all-reduce
  18.2 5.4 all-gather
  23.7 18.2 %all-gather.1 = s32[8,12,2]{1,2,0:T(2,128)S(1)} all-gather(s32[1,12,2]{1,2,0:T(2,128)} %bitcast.156), channel_id=1, replica_groups=mesh['row'=8,'col'=4] {'row'}, dimensions={0}, use_global_device_ids=true | all-gather | bytes 864 | tf_op jit(solution)/shard_map/all_gather | solution.py:64
  43.4 10.5 %all-reduce.3 = (s32[8]{0:T(128)S(1)}, s32[8]{0:T(128)S(1)}) all-reduce(s32[8]{0:T(128)S(1)} %bitcast_dynamic-update-slice_fusion, s32[8]{0:T(128)S(1)} %bitcast_dynamic-update-slice_fusion.1), channel_id=1, replica_groups=mesh['row'=8,'col'=4] {'row'}, use_global_device_ids=true, to_apply=%add.1 | all-reduce | flops 16 | bytes 128
  54.0 38.7 %all-gather.10.cloned.1.call-done = bf16[96,128,128]{2,1,0:T(8,128)(2,1)} async-done(((bf16[12,128,128]{2,1,0:T(8,128)(2,1)}), bf16[96,128,128]{2,1,0:T(8,128)(2,1)}) %all-gather.10.cloned.1.call-update) | async-done | bytes 3145744 | tf_op jit(solution)/shard_map/all_gather | solution.py:63
  92.7 211.2 %while.103 = (s32[]{:T(128)}, f32[12,128,128]{2,1,0:T(8,128)S(1)}, s32[48,2]{0,1:T(2,128)S(1)}, s32[12,2]{0,1:T(2,128)}, s32[4,1]{0,1:T(1,128)S(1)}, /*index=5*/...) while((s32[]{:T(128)}, f32[12,128,128]{2,1,0:T(8,128)S(1)}, ...), condition=%wide.region_7.8_spmd.clone.clone, body=%wide.region_0.7_spmd.clone.sunk.clone | while | flops 34240836 | bytes 5585244 | solution.py:73
  92.7 1.2 constant_dynamic-slice_fusion.30
  96.1 1.1 iota_reduce_fusion.12
  99.7 19.1 %while.102 = (s32[]{:T(128)}, f32[12,128,128]{2,1,0:T(8,128)S(1)}, pred[12,8]{1,0:T(8,128)(4,1)S(1)}, s32[12,8]{1,0:T(8,128)S(1)}, bf16[12,128,128]{2,1,0:T(8,12...) while((s32[]{:T(128)}, f32[12,128,128]{2,1,0:T(8,128)S(1)}, ...), condition=%wide.region_6.6_spmd, body=%wide.region_5.5_spmd.sunk | while | flops 33818672 | bytes 1648009 | solution.py:38
  119.1 1.2 constant_dynamic-slice_fusion.30
  126.1 19.1 %while.102 = (s32[]{:T(128)}, f32[12,128,128]{2,1,0:T(8,128)S(1)}, pred[12,8]{1,0:T(8,128)(4,1)S(1)}, s32[12,8]{1,0:T(8,128)S(1)}, bf16[12,128,128]{2,1,0:T(8,12...) while((s32[]{:T(128)}, f32[12,128,128]{2,1,0:T(8,128)S(1)}, ...), condition=%wide.region_6.6_spmd, body=%wide.region_5.5_spmd.sunk | while | flops 33818672 | bytes 1648009 | solution.py:38
  145.5 1.2 constant_dynamic-slice_fusion.30
  150.8 1.1 iota_reduce_fusion.13
  152.5 19.1 %while.102 = (s32[]{:T(128)}, f32[12,128,128]{2,1,0:T(8,128)S(1)}, pred[12,8]{1,0:T(8,128)(4,1)S(1)}, s32[12,8]{1,0:T(8,128)S(1)}, bf16[12,128,128]{2,1,0:T(8,12...) while((s32[]{:T(128)}, f32[12,128,128]{2,1,0:T(8,128)S(1)}, ...), condition=%wide.region_6.6_spmd, body=%wide.region_5.5_spmd.sunk | while | flops 33818672 | bytes 1648009 | solution.py:38
  171.9 1.2 constant_dynamic-slice_fusion.30
  177.2 1.1 iota_reduce_fusion.13
  178.9 19.1 %while.102 = (s32[]{:T(128)}, f32[12,128,128]{2,1,0:T(8,128)S(1)}, pred[12,8]{1,0:T(8,128)(4,1)S(1)}, s32[12,8]{1,0:T(8,128)S(1)}, bf16[12,128,128]{2,1,0:T(8,12...) while((s32[]{:T(128)}, f32[12,128,128]{2,1,0:T(8,128)S(1)}, ...), condition=%wide.region_6.6_spmd, body=%wide.region_5.5_spmd.sunk | while | flops 33818672 | bytes 1648009 | solution.py:38
  198.3 1.2 constant_dynamic-slice_fusion.30
  203.6 1.1 iota_reduce_fusion.13
  205.3 19.1 %while.102 = (s32[]{:T(128)}, f32[12,128,128]{2,1,0:T(8,128)S(1)}, pred[12,8]{1,0:T(8,128)(4,1)S(1)}, s32[12,8]{1,0:T(8,128)S(1)}, bf16[12,128,128]{2,1,0:T(8,12...) while((s32[]{:T(128)}, f32[12,128,128]{2,1,0:T(8,128)S(1)}, ...), condition=%wide.region_6.6_spmd, body=%wide.region_5.5_spmd.sunk | while | flops 33818672 | bytes 1648009 | solution.py:38
  224.7 1.2 constant_dynamic-slice_fusion.30
  231.7 19.1 %while.102 = (s32[]{:T(128)}, f32[12,128,128]{2,1,0:T(8,128)S(1)}, pred[12,8]{1,0:T(8,128)(4,1)S(1)}, s32[12,8]{1,0:T(8,128)S(1)}, bf16[12,128,128]{2,1,0:T(8,12...) while((s32[]{:T(128)}, f32[12,128,128]{2,1,0:T(8,128)S(1)}, ...), condition=%wide.region_6.6_spmd, body=%wide.region_5.5_spmd.sunk | while | flops 33818672 | bytes 1648009 | solution.py:38
  251.1 1.2 constant_dynamic-slice_fusion.30
  258.1 19.1 %while.102 = (s32[]{:T(128)}, f32[12,128,128]{2,1,0:T(8,128)S(1)}, pred[12,8]{1,0:T(8,128)(4,1)S(1)}, s32[12,8]{1,0:T(8,128)S(1)}, bf16[12,128,128]{2,1,0:T(8,12...) while((s32[]{:T(128)}, f32[12,128,128]{2,1,0:T(8,128)S(1)}, ...), condition=%wide.region_6.6_spmd, body=%wide.region_5.5_spmd.sunk | while | flops 33818672 | bytes 1648009 | solution.py:38
  277.6 1.2 constant_dynamic-slice_fusion.30
  284.5 19.1 %while.102 = (s32[]{:T(128)}, f32[12,128,128]{2,1,0:T(8,128)S(1)}, pred[12,8]{1,0:T(8,128)(4,1)S(1)}, s32[12,8]{1,0:T(8,128)S(1)}, bf16[12,128,128]{2,1,0:T(8,12...) while((s32[]{:T(128)}, f32[12,128,128]{2,1,0:T(8,128)S(1)}, ...), condition=%wide.region_6.6_spmd, body=%wide.region_5.5_spmd.sunk | while | flops 33818672 | bytes 1648009 | solution.py:38
  304.9 15.8 %all-gather.2 = s32[8,12,2]{1,2,0:T(2,128)S(1)} all-gather(s32[1,12,2]{1,2,0:T(2,128)} %bitcast.152), channel_id=1, replica_groups=mesh['row'=8,'col'=4] {'row'}, dimensions={0}, use_global_device_ids=true | all-gather | bytes 864 | tf_op jit(solution)/shard_map/all_gather | solution.py:64
  320.9 1.4 fusion.27
  322.4 42.1 %psum.7 = f32[]{:T(128)} all-reduce(f32[]{:T(128)} %fusion.27), channel_id=1, replica_groups=mesh['row'=8,'col'=4] {'row','col'}, use_global_device_ids=true, to_apply=%region_18.19 | all-reduce | flops 1 | bytes 8 | tf_op jit(solution)/shard_map/psum | solution.py:90
  364.5 211.6 %while.105 = (s32[]{:T(128)}, f32[12,128,128]{2,1,0:T(8,128)S(1)}, s32[48,2]{0,1:T(2,128)S(1)}, s32[12,2]{0,1:T(2,128)}, s32[4,1]{0,1:T(1,128)S(1)}, /*index=5*/...) while((s32[]{:T(128)}, f32[12,128,128]{2,1,0:T(8,128)S(1)}, ...), condition=%wide.region_15.16_spmd.clone.clone, body=%wide.region_8.15_spmd.clone.sunk.clone | while | flops 34240836 | bytes 5585244 | solution.py:73
  364.5 1.2 constant_dynamic-slice_fusion.33
  371.5 19.1 %while.104 = (s32[]{:T(128)}, f32[12,128,128]{2,1,0:T(8,128)S(1)}, pred[12,8]{1,0:T(8,128)(4,1)S(1)}, s32[12,8]{1,0:T(8,128)S(1)}, bf16[12,128,128]{2,1,0:T(8,12...) while((s32[]{:T(128)}, f32[12,128,128]{2,1,0:T(8,128)S(1)}, ...), condition=%wide.region_14.14_spmd, body=%wide.region_13.13_spmd.sunk | while | flops 33818672 | bytes 1648009 | solution.py:38
  390.9 1.2 constant_dynamic-slice_fusion.33
  398.0 19.1 %while.104 = (s32[]{:T(128)}, f32[12,128,128]{2,1,0:T(8,128)S(1)}, pred[12,8]{1,0:T(8,128)(4,1)S(1)}, s32[12,8]{1,0:T(8,128)S(1)}, bf16[12,128,128]{2,1,0:T(8,12...) while((s32[]{:T(128)}, f32[12,128,128]{2,1,0:T(8,128)S(1)}, ...), condition=%wide.region_14.14_spmd, body=%wide.region_13.13_spmd.sunk | while | flops 33818672 | bytes 1648009 | solution.py:38
  417.4 1.2 constant_dynamic-slice_fusion.33
  424.4 19.1 %while.104 = (s32[]{:T(128)}, f32[12,128,128]{2,1,0:T(8,128)S(1)}, pred[12,8]{1,0:T(8,128)(4,1)S(1)}, s32[12,8]{1,0:T(8,128)S(1)}, bf16[12,128,128]{2,1,0:T(8,12...) while((s32[]{:T(128)}, f32[12,128,128]{2,1,0:T(8,128)S(1)}, ...), condition=%wide.region_14.14_spmd, body=%wide.region_13.13_spmd.sunk | while | flops 33818672 | bytes 1648009 | solution.py:38
  443.9 1.2 constant_dynamic-slice_fusion.33
  450.9 19.1 %while.104 = (s32[]{:T(128)}, f32[12,128,128]{2,1,0:T(8,128)S(1)}, pred[12,8]{1,0:T(8,128)(4,1)S(1)}, s32[12,8]{1,0:T(8,128)S(1)}, bf16[12,128,128]{2,1,0:T(8,12...) while((s32[]{:T(128)}, f32[12,128,128]{2,1,0:T(8,128)S(1)}, ...), condition=%wide.region_14.14_spmd, body=%wide.region_13.13_spmd.sunk | while | flops 33818672 | bytes 1648009 | solution.py:38
  470.3 1.2 constant_dynamic-slice_fusion.33
  477.4 19.1 %while.104 = (s32[]{:T(128)}, f32[12,128,128]{2,1,0:T(8,128)S(1)}, pred[12,8]{1,0:T(8,128)(4,1)S(1)}, s32[12,8]{1,0:T(8,128)S(1)}, bf16[12,128,128]{2,1,0:T(8,12...) while((s32[]{:T(128)}, f32[12,128,128]{2,1,0:T(8,128)S(1)}, ...), condition=%wide.region_14.14_spmd, body=%wide.region_13.13_spmd.sunk | while | flops 33818672 | bytes 1648009 | solution.py:38
  496.8 1.2 constant_dynamic-slice_fusion.33
  503.8 19.1 %while.104 = (s32[]{:T(128)}, f32[12,128,128]{2,1,0:T(8,128)S(1)}, pred[12,8]{1,0:T(8,128)(4,1)S(1)}, s32[12,8]{1,0:T(8,128)S(1)}, bf16[12,128,128]{2,1,0:T(8,12...) while((s32[]{:T(128)}, f32[12,128,128]{2,1,0:T(8,128)S(1)}, ...), condition=%wide.region_14.14_spmd, body=%wide.region_13.13_spmd.sunk | while | flops 33818672 | bytes 1648009 | solution.py:38
  523.2 1.2 constant_dynamic-slice_fusion.33
  530.3 19.1 %while.104 = (s32[]{:T(128)}, f32[12,128,128]{2,1,0:T(8,128)S(1)}, pred[12,8]{1,0:T(8,128)(4,1)S(1)}, s32[12,8]{1,0:T(8,128)S(1)}, bf16[12,128,128]{2,1,0:T(8,12...) while((s32[]{:T(128)}, f32[12,128,128]{2,1,0:T(8,128)S(1)}, ...), condition=%wide.region_14.14_spmd, body=%wide.region_13.13_spmd.sunk | while | flops 33818672 | bytes 1648009 | solution.py:38
  549.7 1.2 constant_dynamic-slice_fusion.33
  556.7 19.1 %while.104 = (s32[]{:T(128)}, f32[12,128,128]{2,1,0:T(8,128)S(1)}, pred[12,8]{1,0:T(8,128)(4,1)S(1)}, s32[12,8]{1,0:T(8,128)S(1)}, bf16[12,128,128]{2,1,0:T(8,12...) while((s32[]{:T(128)}, f32[12,128,128]{2,1,0:T(8,128)S(1)}, ...), condition=%wide.region_14.14_spmd, body=%wide.region_13.13_spmd.sunk | while | flops 33818672 | bytes 1648009 | solution.py:38
  (1642 shorter events, 391.5 us)
Async XLA Ops:
  7.2 46.8 %all-gather.8.cloned.1.call-start = ((), (), s32[]{:S(2)}) async-start(), calls=%async_computation | async-start | bytes 1966080 | tf_op jit(solution)/shard_map/all_gather | solution.py:58
  7.9 84.8 %all-gather.10.cloned.1.call-start = ((), (), s32[]{:S(2)}) async-start(), calls=%async_computation.1 | async-start | bytes 3538944 | tf_op jit(solution)/shard_map/all_gather | solution.py:63
  8.6 355.8 %all-gather.14.cloned.1.call-start = ((), (), s32[]{:S(2)}) async-start(), calls=%async_computation.3 | async-start | bytes 3538944 | tf_op jit(solution)/shard_map/all_gather | solution.py:63
  9.4 355.1 %all-gather.12.cloned.1.call-start = ((), (), s32[]{:S(2)}) async-start(), calls=%async_computation.2 | async-start | bytes 1966080 | tf_op jit(solution)/shard_map/all_gather | solution.py:58
Sparse Core Ops, SparseCore 0:
  9.5 19.8 all-gather.7
  31.6 61.0 all-gather.9
  94.9 58.7 all-gather.13
  305.0 17.3 all-gather.11
where the time goes:
time: 585 us; the launch traced here: 584 us
  local copies, waits for them, and re-layouts  279 us (48%)
  blocking collectives  96.4 us (16%)
  other arithmetic  81.8 us (14%)
  matrix products  55.1 us (9%)
  waiting for transfers between devices  40.8 us (7%)
  between operations  15.2 us (3%)
  loops' own time  14.7 us (3%)
    gather x192, local copies, waits for them, and re-layouts, slot_product(): right_vals[right_pick]  115 us
    gather x192, local copies, waits for them, and re-layouts, slot_product(): left_vals[left_pick]  115 us
    dot_general x192, matrix products, slot_product(): jnp.einsum('kxy,kyz->xz', row_blocks, col_blocks, preferred_element_type=...  55.1 us
    psum x1, blocking collectives, per_device(): energy = lax.psum(local_energy, ('row', 'col'))  42.1 us
    all_gather x2, waiting for transfers between devices, multiply(): lax.all_gather(right_tile[0], 'row', axis=0, tiled=True)  38.7 us
    another operation x32, other arithmetic, contribute(): pick_left = jnp.argmax(match_left.astype(jnp.int32), axis=2)  35.9 us
    all_gather x2, blocking collectives, multiply(): lax.all_gather(right_tile[1], 'row', axis=0, tiled=True)  34 us
    dynamic_slice x16, local copies, waits for them, and re-layouts, pick_tile(): vals = lax.dynamic_slice_in_dim(all_vals, start, slot_count, 0)  18.7 us
  transfers between devices with their start and end apart: 4, of which 1 were waited for; matrix products, arithmetic and copies ran while one was open for 36% of the time, Pallas kernels for 0%

commit v1 on v0

--- a/solution.py
+++ b/solution.py
@@ -4,6 +4,28 @@
 from jax.sharding import PartitionSpec as P
 
 TILE = 8
+
+
+def laid_out(blocks, dim):
+    blocks = jnp.moveaxis(blocks, 0, dim)
+    shape = blocks.shape
+    return blocks.reshape(*shape[:dim], shape[dim] * shape[dim + 1], *shape[dim + 2 :])
+
+
+def gather_around(x, axis, dim):
+    size = lax.axis_size(axis)
+    pairs = [(i, (i + 1) % size) for i in range(size)]
+    back = [(b, a) for a, b in pairs]
+    lower, upper = ([], [])
+    for step in range(size - 1):
+        if step % 2 == 0:
+            lower.append(lax.ppermute(lower[-1] if lower else x, axis, pairs))
+        else:
+            upper.append(lax.ppermute(upper[-1] if upper else x, axis, back))
+    blocks = jnp.stack([*lower[::-1], x, *upper])
+    shift = lax.axis_index(axis) - len(lower)
+    blocks = blocks[(jnp.arange(size) - shift) % size]
+    return laid_out(blocks, dim)
 
 
 def contribute(total_sum, left_tile, right_tile, band_index, out_where):
@@ -60,7 +82,7 @@
         lax.all_gather(left_tile[2], "col", axis=0, tiled=True),
     )
     right_all = (
-        lax.all_gather(right_tile[0], "row", axis=0, tiled=True),
+        gather_around(right_tile[0], "row", 0),
         lax.all_gather(right_tile[1], "row", axis=0, tiled=True),
         lax.all_gather(right_tile[2], "row", axis=0, tiled=True),
     )

time: 585 us -> 649 us (1.11)
  waiting for transfers between devices: 40.8 us -> 68.2 us
  starting transfers between devices: 0.15 us -> 27.1 us
  local copies, waits for them, and re-layouts: 279 us -> 291 us
    ppermute x0 -> x14, waiting for transfers between devices: none -> 68.1 us  [the longest x8 42.1 us: gather_around(): lower.append(lax.ppermute(lower[-1] if lower else x, axis, pairs))]
    all_gather x2 -> x0, waiting for transfers between devices: 38.7 us -> none  [multiply(): lax.all_gather(right_tile[0], 'row', axis=0, tiled=True)]
    ppermute x0 -> x14, starting transfers between devices: none -> 27 us  [the longest x6 13.9 us: gather_around(): upper.append(lax.ppermute(upper[-1] if upper else x, axis, back))]
    unnamed x11 -> x37, local copies, waits for them, and re-layouts: 4.75 us -> 19 us
    eq x32, local copies, waits for them, and re-layouts: 12.2 us -> 0.13 us  [contribute(): right_where[None, None, :, 1] == out_where[:, None, None, 1]]
    gather x0 -> x2, local copies, waits for them, and re-layouts: none -> 9.02 us  [gather_around(): blocks = blocks[(jnp.arange(size) - shift) % size]]
  transfers between devices with their start and end apart: 4 -> 16, of which waited for: 1 -> 7; matrix products, arithmetic and copies ran while one was open for 36% -> 35% of each run, Pallas kernels for 0% -> 0%
where the time goes in v1:
time: 649 us; the launch traced here: 648 us
  local copies, waits for them, and re-layouts  291 us (45%)
  blocking collectives  94.8 us (15%)
  other arithmetic  80.5 us (12%)
  waiting for transfers between devices  68.2 us (11%)
  matrix products  55.2 us (9%)
  starting transfers between devices  27.1 us (4%)
  between operations  15.6 us (2%)
  loops' own time  14.8 us (2%)
    gather x192, local copies, waits for them, and re-layouts, slot_product(): left_vals[left_pick]  115 us
    gather x192, local copies, waits for them, and re-layouts, slot_product(): right_vals[right_pick]  115 us
    dot_general x192, matrix products, slot_product(): jnp.einsum('kxy,kyz->xz', row_blocks, col_blocks, preferred_element_type=...  55.2 us
    psum x1, blocking collectives, per_device(): energy = lax.psum(local_energy, ('row', 'col'))  42.2 us
    ppermute x8, waiting for transfers between devices, gather_around(): lower.append(lax.ppermute(lower[-1] if lower else x, axis, pairs))  42.1 us
    another operation x32, other arithmetic, contribute(): pick_left = jnp.argmax(match_left.astype(jnp.int32), axis=2)  35.9 us
    all_gather x2, blocking collectives, multiply(): lax.all_gather(right_tile[1], 'row', axis=0, tiled=True)  31.7 us
    ppermute x6, waiting for transfers between devices, gather_around(): upper.append(lax.ppermute(upper[-1] if upper else x, axis, back))  26 us
  transfers between devices with their start and end apart: 16, of which 7 were waited for; matrix products, arithmetic and copies ran while one was open for 35% of the time, Pallas kernels for 0%

profile of v1, /device:TPU:12, one launch (start us, length us, event | category | flops | bytes accessed | tf_op | source)
XLA Modules:
  0.0 647.5 jit_solution(5085493821582999186)
XLA Ops:
  7.2 1.5 collective-permute-start
  8.8 1.5 collective-permute-start.7
  10.3 10.1 %collective-permute-done = bf16[12,128,128]{2,1,0:T(8,128)(2,1)S(1)} collective-permute-done((bf16[12,128,128]{2,1,0:T(8,128)(2,1)}, bf16[12,128,128]{2,1,0:T(8,128)(2,1)S(1)}, u32[]{:S(2)}, u32[]{:S(2)}) %collective-permute-start) | collective-permute-done | bytes 393248 | tf_op jit(solution)/shard_map/ppermute | solution.py:22
  21.0 2.3 collective-permute-start.4
  23.3 12.1 %collective-permute-done.7 = bf16[12,128,128]{2,1,0:T(8,128)(2,1)S(1)} collective-permute-done((bf16[12,128,128]{2,1,0:T(8,128)(2,1)}, bf16[12,128,128]{2,1,0:T(8,128)(2,1)S(1)}, u32[]{:S(2)}, u32[]{:S(2)}) %collective-permute-start.7) | collective-permute-done | bytes 393248 | tf_op jit(solution)/shard_map/ppermute | solution.py:22
  35.4 2.4 collective-permute-start.8
  37.8 5.9 collective-permute-done.1
  43.8 2.5 collective-permute-start.2
  46.8 14.7 %collective-permute-done.4 = bf16[12,128,128]{2,1,0:T(8,128)(2,1)S(1)} collective-permute-done((bf16[12,128,128]{2,1,0:T(8,128)(2,1)}, bf16[12,128,128]{2,1,0:T(8,128)(2,1)S(1)}, u32[]{:S(2)}, u32[]{:S(2)}) %collective-permute-start.4) | collective-permute-done | bytes 393248 | tf_op jit(solution)/shard_map/ppermute | solution.py:24
  61.5 1.4 collective-permute-start.5
  63.5 14.0 %collective-permute-done.2 = bf16[12,128,128]{2,1,0:T(8,128)(2,1)} collective-permute-done((bf16[12,128,128]{2,1,0:T(8,128)(2,1)S(1)}, bf16[12,128,128]{2,1,0:T(8,128)(2,1)}, u32[]{:S(2)}, u32[]{:S(2)}) %collective-permute-start.2) | collective-permute-done | bytes 393248 | tf_op jit(solution)/shard_map/ppermute | solution.py:22
  77.5 2.6 collective-permute-start.3
  81.4 1.2 dynamic-slice.1
  82.6 1.2 dynamic-slice
  85.9 4.3 all-reduce
  90.2 11.3 %all-reduce.3 = (s32[8]{0:T(128)S(1)}, s32[8]{0:T(128)S(1)}) all-reduce(s32[8]{0:T(128)S(1)} %bitcast_dynamic-update-slice_fusion.16, s32[8]{0:T(128)S(1)} %bitcast_dynamic-update-slice_fusion.17), channel_id=1, replica_groups=mesh['row'=8,'col'=4] {'row'}, use_global_device_ids=true, to_apply=%add.1 | all-reduce | flops 16 | bytes 128
  101.5 5.3 all-gather
  106.8 15.4 %all-gather.1 = s32[8,12,2]{1,2,0:T(2,128)S(1)} all-gather(s32[1,12,2]{1,2,0:T(2,128)} %bitcast.194), channel_id=1, replica_groups=mesh['row'=8,'col'=4] {'row'}, dimensions={0}, use_global_device_ids=true | all-gather | bytes 864 | tf_op jit(solution)/shard_map/all_gather | solution.py:86
  122.4 4.1 collective-permute-start.12
  127.2 1.4 collective-permute-start.10
  128.6 1.8 bitcast_dynamic-update-slice_fusion.15
  130.3 1.8 bitcast_dynamic-update-slice_fusion.14
  135.2 1.8 bitcast_dynamic-update-slice_fusion.9
  137.0 10.1 %collective-permute-done.6 = bf16[12,128,128]{2,1,0:T(8,128)(2,1)S(1)} collective-permute-done((bf16[12,128,128]{2,1,0:T(8,128)(2,1)}, bf16[12,128,128]{2,1,0:T(8,128)(2,1)S(1)}, u32[]{:S(2)}, u32[]{:S(2)}) %collective-permute-start.6) | collective-permute-done | bytes 393248 | tf_op jit(solution)/shard_map/ppermute | solution.py:24
  147.9 4.5 gather_fusion.4
  152.4 204.4 %while.103 = (s32[]{:T(128)}, f32[12,128,128]{2,1,0:T(8,128)S(1)}, s32[48,2]{0,1:T(2,128)S(1)}, s32[12,2]{0,1:T(2,128)S(1)}, s32[4,1]{0,1:T(1,128)S(1)}, /*index...) while((s32[]{:T(128)}, f32[12,128,128]{2,1,0:T(8,128)S(1)}, ...), condition=%wide.region_7.8_spmd.clone.clone, body=%wide.region_0.7_spmd.clone.sunk.clone | while | flops 34240836 | bytes 5585244 | solution.py:95
  158.6 19.1 %while.102 = (s32[]{:T(128)}, f32[12,128,128]{2,1,0:T(8,128)S(1)}, pred[12,8]{1,0:T(8,128)(4,1)S(1)}, s32[12,8]{1,0:T(8,128)S(1)}, bf16[12,128,128]{2,1,0:T(8,12...) while((s32[]{:T(128)}, f32[12,128,128]{2,1,0:T(8,128)S(1)}, ...), condition=%wide.region_6.6_spmd, body=%wide.region_5.5_spmd.sunk | while | flops 33818672 | bytes 1648009 | solution.py:60
  184.1 19.1 %while.102 = (s32[]{:T(128)}, f32[12,128,128]{2,1,0:T(8,128)S(1)}, pred[12,8]{1,0:T(8,128)(4,1)S(1)}, s32[12,8]{1,0:T(8,128)S(1)}, bf16[12,128,128]{2,1,0:T(8,12...) while((s32[]{:T(128)}, f32[12,128,128]{2,1,0:T(8,128)S(1)}, ...), condition=%wide.region_6.6_spmd, body=%wide.region_5.5_spmd.sunk | while | flops 33818672 | bytes 1648009 | solution.py:60
  209.7 19.1 %while.102 = (s32[]{:T(128)}, f32[12,128,128]{2,1,0:T(8,128)S(1)}, pred[12,8]{1,0:T(8,128)(4,1)S(1)}, s32[12,8]{1,0:T(8,128)S(1)}, bf16[12,128,128]{2,1,0:T(8,12...) while((s32[]{:T(128)}, f32[12,128,128]{2,1,0:T(8,128)S(1)}, ...), condition=%wide.region_6.6_spmd, body=%wide.region_5.5_spmd.sunk | while | flops 33818672 | bytes 1648009 | solution.py:60
  235.2 19.1 %while.102 = (s32[]{:T(128)}, f32[12,128,128]{2,1,0:T(8,128)S(1)}, pred[12,8]{1,0:T(8,128)(4,1)S(1)}, s32[12,8]{1,0:T(8,128)S(1)}, bf16[12,128,128]{2,1,0:T(8,12...) while((s32[]{:T(128)}, f32[12,128,128]{2,1,0:T(8,128)S(1)}, ...), condition=%wide.region_6.6_spmd, body=%wide.region_5.5_spmd.sunk | while | flops 33818672 | bytes 1648009 | solution.py:60
  260.8 19.1 %while.102 = (s32[]{:T(128)}, f32[12,128,128]{2,1,0:T(8,128)S(1)}, pred[12,8]{1,0:T(8,128)(4,1)S(1)}, s32[12,8]{1,0:T(8,128)S(1)}, bf16[12,128,128]{2,1,0:T(8,12...) while((s32[]{:T(128)}, f32[12,128,128]{2,1,0:T(8,128)S(1)}, ...), condition=%wide.region_6.6_spmd, body=%wide.region_5.5_spmd.sunk | while | flops 33818672 | bytes 1648009 | solution.py:60
  286.3 19.1 %while.102 = (s32[]{:T(128)}, f32[12,128,128]{2,1,0:T(8,128)S(1)}, pred[12,8]{1,0:T(8,128)(4,1)S(1)}, s32[12,8]{1,0:T(8,128)S(1)}, bf16[12,128,128]{2,1,0:T(8,12...) while((s32[]{:T(128)}, f32[12,128,128]{2,1,0:T(8,128)S(1)}, ...), condition=%wide.region_6.6_spmd, body=%wide.region_5.5_spmd.sunk | while | flops 33818672 | bytes 1648009 | solution.py:60
  311.9 19.1 %while.102 = (s32[]{:T(128)}, f32[12,128,128]{2,1,0:T(8,128)S(1)}, pred[12,8]{1,0:T(8,128)(4,1)S(1)}, s32[12,8]{1,0:T(8,128)S(1)}, bf16[12,128,128]{2,1,0:T(8,12...) while((s32[]{:T(128)}, f32[12,128,128]{2,1,0:T(8,128)S(1)}, ...), condition=%wide.region_6.6_spmd, body=%wide.region_5.5_spmd.sunk | while | flops 33818672 | bytes 1648009 | solution.py:60
  337.5 19.1 %while.102 = (s32[]{:T(128)}, f32[12,128,128]{2,1,0:T(8,128)S(1)}, pred[12,8]{1,0:T(8,128)(4,1)S(1)}, s32[12,8]{1,0:T(8,128)S(1)}, bf16[12,128,128]{2,1,0:T(8,12...) while((s32[]{:T(128)}, f32[12,128,128]{2,1,0:T(8,128)S(1)}, ...), condition=%wide.region_6.6_spmd, body=%wide.region_5.5_spmd.sunk | while | flops 33818672 | bytes 1648009 | solution.py:60
  357.8 16.3 %all-gather.2 = s32[8,12,2]{1,2,0:T(2,128)S(1)} all-gather(s32[1,12,2]{1,2,0:T(2,128)S(1)} %bitcast.190), channel_id=1, replica_groups=mesh['row'=8,'col'=4] {'row'}, dimensions={0}, use_global_device_ids=true | all-gather | bytes 864 | tf_op jit(solution)/shard_map/all_gather | solution.py:86
  374.2 4.9 collective-permute-start.13
  385.0 1.4 copy-done
  387.1 4.5 gather_fusion.5
  391.6 42.2 %psum.7 = f32[]{:T(128)} all-reduce(f32[]{:T(128)} %fusion.29), channel_id=1, replica_groups=mesh['row'=8,'col'=4] {'row','col'}, use_global_device_ids=true, to_apply=%region_18.19 | all-reduce | flops 1 | bytes 8 | tf_op jit(solution)/shard_map/psum | solution.py:112
  433.8 206.0 %while.105 = (s32[]{:T(128)}, f32[12,128,128]{2,1,0:T(8,128)S(1)}, s32[48,2]{0,1:T(2,128)S(1)}, s32[12,2]{0,1:T(2,128)S(1)}, s32[4,1]{0,1:T(1,128)S(1)}, /*index...) while((s32[]{:T(128)}, f32[12,128,128]{2,1,0:T(8,128)S(1)}, ...), condition=%wide.region_15.16_spmd.clone.clone, body=%wide.region_8.15_spmd.clone.sunk.clone | while | flops 34240836 | bytes 5585244 | solution.py:95
  440.1 19.1 %while.104 = (s32[]{:T(128)}, f32[12,128,128]{2,1,0:T(8,128)S(1)}, pred[12,8]{1,0:T(8,128)(4,1)S(1)}, s32[12,8]{1,0:T(8,128)S(1)}, bf16[12,128,128]{2,1,0:T(8,12...) while((s32[]{:T(128)}, f32[12,128,128]{2,1,0:T(8,128)S(1)}, ...), condition=%wide.region_14.14_spmd, body=%wide.region_13.13_spmd.sunk | while | flops 33818672 | bytes 1648009 | solution.py:60
  465.9 19.1 %while.104 = (s32[]{:T(128)}, f32[12,128,128]{2,1,0:T(8,128)S(1)}, pred[12,8]{1,0:T(8,128)(4,1)S(1)}, s32[12,8]{1,0:T(8,128)S(1)}, bf16[12,128,128]{2,1,0:T(8,12...) while((s32[]{:T(128)}, f32[12,128,128]{2,1,0:T(8,128)S(1)}, ...), condition=%wide.region_14.14_spmd, body=%wide.region_13.13_spmd.sunk | while | flops 33818672 | bytes 1648009 | solution.py:60
  491.6 19.1 %while.104 = (s32[]{:T(128)}, f32[12,128,128]{2,1,0:T(8,128)S(1)}, pred[12,8]{1,0:T(8,128)(4,1)S(1)}, s32[12,8]{1,0:T(8,128)S(1)}, bf16[12,128,128]{2,1,0:T(8,12...) while((s32[]{:T(128)}, f32[12,128,128]{2,1,0:T(8,128)S(1)}, ...), condition=%wide.region_14.14_spmd, body=%wide.region_13.13_spmd.sunk | while | flops 33818672 | bytes 1648009 | solution.py:60
  517.4 19.1 %while.104 = (s32[]{:T(128)}, f32[12,128,128]{2,1,0:T(8,128)S(1)}, pred[12,8]{1,0:T(8,128)(4,1)S(1)}, s32[12,8]{1,0:T(8,128)S(1)}, bf16[12,128,128]{2,1,0:T(8,12...) while((s32[]{:T(128)}, f32[12,128,128]{2,1,0:T(8,128)S(1)}, ...), condition=%wide.region_14.14_spmd, body=%wide.region_13.13_spmd.sunk | while | flops 33818672 | bytes 1648009 | solution.py:60
  543.2 19.1 %while.104 = (s32[]{:T(128)}, f32[12,128,128]{2,1,0:T(8,128)S(1)}, pred[12,8]{1,0:T(8,128)(4,1)S(1)}, s32[12,8]{1,0:T(8,128)S(1)}, bf16[12,128,128]{2,1,0:T(8,12...) while((s32[]{:T(128)}, f32[12,128,128]{2,1,0:T(8,128)S(1)}, ...), condition=%wide.region_14.14_spmd, body=%wide.region_13.13_spmd.sunk | while | flops 33818672 | bytes 1648009 | solution.py:60
  568.9 19.1 %while.104 = (s32[]{:T(128)}, f32[12,128,128]{2,1,0:T(8,128)S(1)}, pred[12,8]{1,0:T(8,128)(4,1)S(1)}, s32[12,8]{1,0:T(8,128)S(1)}, bf16[12,128,128]{2,1,0:T(8,12...) while((s32[]{:T(128)}, f32[12,128,128]{2,1,0:T(8,128)S(1)}, ...), condition=%wide.region_14.14_spmd, body=%wide.region_13.13_spmd.sunk | while | flops 33818672 | bytes 1648009 | solution.py:60
  594.7 19.1 %while.104 = (s32[]{:T(128)}, f32[12,128,128]{2,1,0:T(8,128)S(1)}, pred[12,8]{1,0:T(8,128)(4,1)S(1)}, s32[12,8]{1,0:T(8,128)S(1)}, bf16[12,128,128]{2,1,0:T(8,12...) while((s32[]{:T(128)}, f32[12,128,128]{2,1,0:T(8,128)S(1)}, ...), condition=%wide.region_14.14_spmd, body=%wide.region_13.13_spmd.sunk | while | flops 33818672 | bytes 1648009 | solution.py:60
  620.4 19.1 %while.104 = (s32[]{:T(128)}, f32[12,128,128]{2,1,0:T(8,128)S(1)}, pred[12,8]{1,0:T(8,128)(4,1)S(1)}, s32[12,8]{1,0:T(8,128)S(1)}, bf16[12,128,128]{2,1,0:T(8,12...) while((s32[]{:T(128)}, f32[12,128,128]{2,1,0:T(8,128)S(1)}, ...), condition=%wide.region_14.14_spmd, body=%wide.region_13.13_spmd.sunk | while | flops 33818672 | bytes 1648009 | solution.py:60
  (1696 shorter events, 412.6 us)
Async XLA Ops:
  7.2 126.5 %copy-start.2 = (bf16[12,128,128]{2,1,0:T(8,128)(2,1)S(1)}, bf16[12,128,128]{2,1,0:T(8,128)(2,1)}, u32[]{:S(2)}) copy-start(bf16[12,128,128]{2,1,0:T(8,128)(2,1)} %param.17) | copy-start | bytes 1179652
  7.2 145.2 %all-gather.6.cloned.1.call-start = ((), (), s32[]{:S(2)}) async-start(), calls=%async_computation | async-start | bytes 1966080 | tf_op jit(solution)/shard_map/all_gather | solution.py:80
  7.2 13.1 %collective-permute-start = (bf16[12,128,128]{2,1,0:T(8,128)(2,1)}, bf16[12,128,128]{2,1,0:T(8,128)(2,1)S(1)}, u32[]{:S(2)}, u32[]{:S(2)}) collective-permute-start(bf16[12,128,128]{2,1,0:T(8,128)(2,1)} %param.17), channel_id=1, source_target_pairs={{0,4},{4,8},{8,12},{12,16},{16,20},{20,24},{24,28},{28,0},{1,5},{5... | collective-permute-start | bytes 1179656 | tf_op jit(solution)/shard_map/ppermute | solution.py:22
  8.8 26.7 %collective-permute-start.7 = (bf16[12,128,128]{2,1,0:T(8,128)(2,1)}, bf16[12,128,128]{2,1,0:T(8,128)(2,1)S(1)}, u32[]{:S(2)}, u32[]{:S(2)}) collective-permute-start(bf16[12,128,128]{2,1,0:T(8,128)(2,1)} %param.14), channel_id=1, source_target_pairs={{0,4},{4,8},{8,12},{12,16},{16,20},{20,24},{24,28},{28,0},{1,5},{5... | collective-permute-start | bytes 1179656 | tf_op jit(solution)/shard_map/ppermute | solution.py:22
  20.4 23.4 %collective-permute-start.1 = (bf16[12,128,128]{2,1,0:T(8,128)(2,1)S(1)}, bf16[12,128,128]{2,1,0:T(8,128)(2,1)S(1)}, u32[]{:S(2)}, u32[]{:S(2)}) collective-permute-start(bf16[12,128,128]{2,1,0:T(8,128)(2,1)S(1)} %collective-permute-done), channel_id=1, source_target_pairs={{0,4},{4,8},{8,12},{12,16},{16,20},{20,24},{24,28},{28,0},{1,5},{5... | collective-permute-start | bytes 1179656 | tf_op jit(solution)/shard_map/ppermute | solution.py:22
  21.0 40.5 %collective-permute-start.4 = (bf16[12,128,128]{2,1,0:T(8,128)(2,1)}, bf16[12,128,128]{2,1,0:T(8,128)(2,1)S(1)}, u32[]{:S(2)}, u32[]{:S(2)}) collective-permute-start(bf16[12,128,128]{2,1,0:T(8,128)(2,1)} %param.17), channel_id=1, source_target_pairs={{4,0},{8,4},{12,8},{16,12},{20,16},{24,20},{28,24},{0,28},{5,1},{9... | collective-permute-start | bytes 1179656 | tf_op jit(solution)/shard_map/ppermute | solution.py:24
  35.4 27.5 %collective-permute-start.8 = (bf16[12,128,128]{2,1,0:T(8,128)(2,1)S(1)}, bf16[12,128,128]{2,1,0:T(8,128)(2,1)S(1)}, u32[]{:S(2)}, u32[]{:S(2)}) collective-permute-start(bf16[12,128,128]{2,1,0:T(8,128)(2,1)S(1)} %collective-permute-done.7), channel_id=1, source_target_pairs={{0,4},{4,8},{8,12},{12,16},{16,20},{20,24},{24,28},{28,0},{1,5},{5... | collective-permute-start | bytes 1179656 | tf_op jit(solution)/shard_map/ppermute | solution.py:22
  43.8 33.7 %collective-permute-start.2 = (bf16[12,128,128]{2,1,0:T(8,128)(2,1)S(1)}, bf16[12,128,128]{2,1,0:T(8,128)(2,1)}, u32[]{:S(2)}, u32[]{:S(2)}) collective-permute-start(bf16[12,128,128]{2,1,0:T(8,128)(2,1)S(1)} %collective-permute-done.1), channel_id=1, source_target_pairs={{0,4},{4,8},{8,12},{12,16},{16,20},{20,24},{24,28},{28,0},{1,5},{5... | collective-permute-start | bytes 1179656 | tf_op jit(solution)/shard_map/ppermute | solution.py:22
  46.3 387.5 %all-gather.8.cloned.1.call-start = ((), (), s32[]{:S(2)}) async-start(), calls=%async_computation.1 | async-start | bytes 1966080 | tf_op jit(solution)/shard_map/all_gather | solution.py:80
  46.3 76.1 %collective-permute-start.11 = (bf16[12,128,128]{2,1,0:T(8,128)(2,1)}, bf16[12,128,128]{2,1,0:T(8,128)(2,1)}, u32[]{:S(2)}, u32[]{:S(2)}) collective-permute-start(bf16[12,128,128]{2,1,0:T(8,128)(2,1)} %param.14), channel_id=1, source_target_pairs={{4,0},{8,4},{12,8},{16,12},{20,16},{24,20},{28,24},{0,28},{5,1},{9... | collective-permute-start | bytes 1179656 | tf_op jit(solution)/shard_map/ppermute | solution.py:24
  61.5 65.1 %collective-permute-start.5 = (bf16[12,128,128]{2,1,0:T(8,128)(2,1)S(1)}, bf16[12,128,128]{2,1,0:T(8,128)(2,1)}, u32[]{:S(2)}, u32[]{:S(2)}) collective-permute-start(bf16[12,128,128]{2,1,0:T(8,128)(2,1)S(1)} %collective-permute-done.4), channel_id=1, source_target_pairs={{4,0},{8,4},{12,8},{16,12},{20,16},{24,20},{28,24},{0,28},{5,1},{9... | collective-permute-start | bytes 1179656 | tf_op jit(solution)/shard_map/ppermute | solution.py:24
  62.9 85.0 %copy-start.3 = (bf16[12,128,128]{2,1,0:T(8,128)(2,1)}, bf16[12,128,128]{2,1,0:T(8,128)(2,1)S(1)}, u32[]{:S(2)}) copy-start(bf16[12,128,128]{2,1,0:T(8,128)(2,1)S(1)} %collective-permute-done.8) | copy-start | bytes 1179652
  62.9 64.3 %collective-permute-start.9 = (bf16[12,128,128]{2,1,0:T(8,128)(2,1)S(1)}, bf16[12,128,128]{2,1,0:T(8,128)(2,1)}, u32[]{:S(2)}, u32[]{:S(2)}) collective-permute-start(bf16[12,128,128]{2,1,0:T(8,128)(2,1)S(1)} %collective-permute-done.8), channel_id=1, source_target_pairs={{0,4},{4,8},{8,12},{12,16},{16,20},{20,24},{24,28},{28,0},{1,5},{5... | collective-permute-start | bytes 1179656 | tf_op jit(solution)/shard_map/ppermute | solution.py:22
  77.5 51.1 %collective-permute-start.3 = (bf16[12,128,128]{2,1,0:T(8,128)(2,1)}, bf16[12,128,128]{2,1,0:T(8,128)(2,1)}, u32[]{:S(2)}, u32[]{:S(2)}) collective-permute-start(bf16[12,128,128]{2,1,0:T(8,128)(2,1)} %collective-permute-done.2), channel_id=1, source_target_pairs={{0,4},{4,8},{8,12},{12,16},{16,20},{20,24},{24,28},{28,0},{1,5},{5... | collective-permute-start | bytes 1179656 | tf_op jit(solution)/shard_map/ppermute | solution.py:22
  122.4 251.8 %collective-permute-start.12 = (bf16[12,128,128]{2,1,0:T(8,128)(2,1)}, bf16[12,128,128]{2,1,0:T(8,128)(2,1)}, u32[]{:S(2)}, u32[]{:S(2)}) collective-permute-start(bf16[12,128,128]{2,1,0:T(8,128)(2,1)} %collective-permute-done.11), channel_id=1, source_target_pairs={{4,0},{8,4},{12,8},{16,12},{20,16},{24,20},{28,24},{0,28},{5,1},{9... | collective-permute-start | bytes 1179656 | tf_op jit(solution)/shard_map/ppermute | solution.py:24
  126.5 20.6 %collective-permute-start.6 = (bf16[12,128,128]{2,1,0:T(8,128)(2,1)}, bf16[12,128,128]{2,1,0:T(8,128)(2,1)S(1)}, u32[]{:S(2)}, u32[]{:S(2)}) collective-permute-start(bf16[12,128,128]{2,1,0:T(8,128)(2,1)} %collective-permute-done.5), channel_id=1, source_target_pairs={{4,0},{8,4},{12,8},{16,12},{20,16},{24,20},{28,24},{0,28},{5,1},{9... | collective-permute-start | bytes 1179656 | tf_op jit(solution)/shard_map/ppermute | solution.py:24
  127.2 251.9 %collective-permute-start.10 = (bf16[12,128,128]{2,1,0:T(8,128)(2,1)}, bf16[12,128,128]{2,1,0:T(8,128)(2,1)}, u32[]{:S(2)}, u32[]{:S(2)}) collective-permute-start(bf16[12,128,128]{2,1,0:T(8,128)(2,1)} %collective-permute-done.9), channel_id=1, source_target_pairs={{0,4},{4,8},{8,12},{12,16},{16,20},{20,24},{24,28},{28,0},{1,5},{5... | collective-permute-start | bytes 1179656 | tf_op jit(solution)/shard_map/ppermute | solution.py:22
  147.9 4.5 copy-start.5
  356.9 24.3 %copy-start.4 = (bf16[12,128,128]{2,1,0:T(8,128)(2,1)S(1)}, bf16[12,128,128]{2,1,0:T(8,128)(2,1)}, u32[]{:S(2)}) copy-start(bf16[12,128,128]{2,1,0:T(8,128)(2,1)} %copy-done.3) | copy-start | bytes 1179652
  356.9 24.4 %copy-start.1 = (bf16[12,128,128]{2,1,0:T(8,128)(2,1)S(1)}, bf16[12,128,128]{2,1,0:T(8,128)(2,1)}, u32[]{:S(2)}) copy-start(bf16[12,128,128]{2,1,0:T(8,128)(2,1)} %param.14) | copy-start | bytes 1179652
  374.2 10.5 %collective-permute-start.13 = (bf16[12,128,128]{2,1,0:T(8,128)(2,1)}, bf16[12,128,128]{2,1,0:T(8,128)(2,1)S(1)}, u32[]{:S(2)}, u32[]{:S(2)}) collective-permute-start(bf16[12,128,128]{2,1,0:T(8,128)(2,1)} %collective-permute-done.12), channel_id=1, source_target_pairs={{4,0},{8,4},{12,8},{16,12},{20,16},{24,20},{28,24},{0,28},{5,1},{9... | collective-permute-start | bytes 1179656 | tf_op jit(solution)/shard_map/ppermute | solution.py:24
  384.8 1.7 copy-start
Sparse Core Ops, SparseCore 0:
  46.4 18.8 all-gather.5
  357.9 18.6 all-gather.7
